TPU v7x, 256 devices: a whole 4x4x8 slice. The times are simulated.
256 devices in a mesh: band: 16 (over x_lo, z), slab: 16 (over y, x_hi, core).
Axes of the slice: x: 4 (x_hi: 2, x_lo: 2; x = x_hi * 2 + x_lo), y: 4, z: 8, core: 2. Of those that a mesh axis runs over, the one named last changes fastest.
Arguments:
- orbitals: float32 [256, 48, 2304], P('band', 'slab'), may hold values from -6 to 6
- partners: int32 [16, 2], replicated, may hold values from 0 to 15, as said below
- counts: int32 [16, 2], replicated, may hold values from 1 to 16
Outputs:
- forces: float32 [256, 48, 2304], P('band', 'slab')
- energy: float32 [], replicated
Inputs may be any that keep to these rules, and one draw needn't show every extreme that they name: `partners`: row g names two different band groups, neither of them g.
All inputs are finite; a program needn't handle non-finite values.
Results may differ from a plain program's by a relative error of at most 0.0001.
Values sent between devices are 32-bit elements; how exact they have to be, the bound alone decides.
A program may use at most 64 MiB of HBM per device.

v0:
```python
import functools
import math
import jax
import jax.numpy as jnp
from jax import lax
from jax.sharding import Mesh
from jax.sharding import PartitionSpec as P

NX = 48
NY = 48
NZ = 48
NZP = 96
BAND = ("band_0", "band_1")
SLAB = ("slab_0", "slab_1", "slab_2")
BAND_SLAB = ("band_0", "band_1", "slab_0", "slab_1", "slab_2")
slater_coeff = -((3.0 / math.pi) ** (1.0 / 3.0))
exchange_mix = 0.25
screening = 0.25
highest = lax.Precision.HIGHEST


def over_axes(value, axes):
    return functools.reduce(lax.psum, axes, value)


def dft_block(count_in, count_out, length, sign):
    row_iota = lax.broadcasted_iota(jnp.int32, (count_in, count_out), 0)
    col_iota = lax.broadcasted_iota(jnp.int32, (count_in, count_out), 1)
    phase_angle = 2.0 * math.pi / length * (row_iota * col_iota % length).astype(jnp.float32)
    cosine = jnp.cos(phase_angle)
    sine = jnp.sin(phase_angle)
    upper = jnp.stack([cosine, -sign * sine])
    lower = jnp.stack([sign * sine, cosine])
    return jnp.stack([upper, lower])


def wavenumber_sq(length):
    position = jnp.arange(length, dtype=jnp.int32)
    signed = jnp.where(position > length // 2, position - length, position).astype(jnp.float32)
    wave_number = 2.0 * math.pi / length * signed
    return wave_number * wave_number


def screened_potential(fields):
    spectrum = jnp.einsum(
        "coxyz,cdzk->doxyk", fields, dft_block(NZ, NZP, NZP, 1.0), precision=highest
    )
    spectrum = jnp.einsum(
        "coxyk,cdyq->doxqk", spectrum, dft_block(NY, NY, NY, 1.0), precision=highest
    )
    spectrum = jnp.einsum(
        "coxqk,cdxp->dopqk", spectrum, dft_block(NX, NX, NX, 1.0), precision=highest
    )
    total = (
        wavenumber_sq(NX)[:, None, None]
        + wavenumber_sq(NY)[None, :, None]
        + wavenumber_sq(NZP)[None, None, :]
    )
    kernel_table = 4.0 * math.pi / (NX * NY * NZP) / (total + screening * screening)
    spectrum = spectrum * kernel_table
    spectrum = jnp.einsum(
        "copqk,cdpx->doxqk", spectrum, dft_block(NX, NX, NX, -1.0), precision=highest
    )
    spectrum = jnp.einsum(
        "coxqk,cdqy->doxyk", spectrum, dft_block(NY, NY, NY, -1.0), precision=highest
    )
    return jnp.einsum(
        "coxyk,cdkz->doxyz", spectrum, dft_block(NZP, NZ, NZP, -1.0), precision=highest
    )


def pair_terms(own_orbs, visitors, active):
    per_device = own_orbs.shape[0]
    pair_density = own_orbs[None] * visitors * active[:, :, None, None]
    shaped = pair_density.reshape(2, per_device, NX, NY, NZ)
    fields = screened_potential(shaped).reshape(pair_density.shape)
    own_force = -exchange_mix * jnp.sum(fields * visitors, axis=0)
    partner_force = -exchange_mix * fields * own_orbs[None]
    energy_term = jnp.sum(pair_density * fields)
    return (own_force, partner_force, energy_term)


def request_rows(held_rows, partners, width):
    row_index = (partners[:, :, None] * width + jnp.arange(width, dtype=jnp.int32)).reshape(-1)
    return jnp.take(held_rows, row_index, axis=0)


def return_rows(pieces, partners, bands):
    flat = pieces.reshape(bands * 2, -1)
    targets = jnp.arange(bands, dtype=jnp.int32)[:, None]
    onehot = (partners.reshape(-1)[None, :] == targets).astype(jnp.float32)
    summed = jnp.dot(onehot, flat, precision=highest)
    width = pieces.shape[0] // (bands * 2)
    return summed.reshape((bands * width,) + pieces.shape[1:])


def body(orbitals, partners, counts):
    bands = lax.axis_size(BAND)
    slabs = lax.axis_size(SLAB)
    band_index = lax.axis_index(BAND)
    slab_index = lax.axis_index(SLAB)
    orb_group = orbitals.shape[0]
    per_device = orb_group // slabs
    total_orbs = orb_group * bands
    squares = jnp.sum(orbitals * orbitals, axis=0)
    density = 2.0 / total_orbs * over_axes(squares, BAND)
    local_pot = slater_coeff * jnp.cbrt(density)
    band_match = jnp.arange(bands, dtype=jnp.int32)[:, None] == band_index
    my_counts = jnp.sum(jnp.where(band_match, counts, 0), axis=0)
    local_rows = slab_index * per_device + jnp.arange(per_device, dtype=jnp.int32)
    active = (local_rows[None, :] < my_counts[:, None]).astype(jnp.float32)
    own_orbs = lax.all_to_all(orbitals, SLAB, split_axis=0, concat_axis=1, tiled=True)
    held_rows = lax.all_to_all(own_orbs, BAND, split_axis=1, concat_axis=0, tiled=True)
    wanted = request_rows(held_rows, partners, per_device)
    visitors = lax.all_to_all(wanted, BAND, split_axis=0, concat_axis=1, tiled=True)
    visitors = visitors.reshape((2, per_device) + own_orbs.shape[1:])
    own_force, partner_force, energy_term = pair_terms(own_orbs, visitors, active)
    outgoing = partner_force.reshape((2 * per_device,) + own_orbs.shape[1:])
    outgoing = lax.all_to_all(outgoing, BAND, split_axis=1, concat_axis=0, tiled=True)
    returned = lax.all_to_all(
        return_rows(outgoing, partners, bands), BAND, split_axis=0, concat_axis=1, tiled=True
    )
    exchange_force = lax.all_to_all(
        own_force + returned, SLAB, split_axis=1, concat_axis=0, tiled=True
    )
    energy_total = over_axes(energy_term, BAND_SLAB)
    energy = -energy_total / (2.0 * total_orbs * NX * NY * NZ)
    forces = local_pot[None] * orbitals + exchange_force
    return (forces, energy)


def solution(mesh):
    torus = Mesh(
        mesh.devices.reshape(2, 8, 4, 2, 2), ("band_0", "band_1", "slab_0", "slab_1", "slab_2")
    )
    in_specs = (P(BAND, SLAB, None), P(), P())
    out_specs = (P(BAND, SLAB, None), P())
    return jax.shard_map(body, mesh=torus, in_specs=in_specs, out_specs=out_specs, check_vma=False)
```

profile of v0, /device:TPU:1, one launch (start us, length us, event | category | flops | bytes accessed | tf_op | source)
XLA Modules:
  0.0 241.4 jit_solution(8340046165394980093)
XLA Ops:
  2.8 8.4 %all-to-all-start = ((f32[16,3,2304]{2,1,0:T(4,128)}), f32[16,3,2304]{2,1,0:T(4,128)S(1)}, u32[]{:S(2)}, u32[]{:S(2)}) async-start(f32[16,3,2304]{2,1,0:T(4,128)} %copy.93), calls=%async_computation | async-start | bytes 1179648 | tf_op jit(solution)/shard_map/all_to_all | solution.py:112
  13.1 9.9 %all-to-all-done = f32[16,3,2304]{2,1,0:T(4,128)S(1)} async-done(((f32[16,3,2304]{2,1,0:T(4,128)}), f32[16,3,2304]{2,1,0:T(4,128)S(1)}, u32[]{:S(2)}, u32[]{:S(2)}) %all-to-all-start) | async-done | bytes 442400 | tf_op jit(solution)/shard_map/all_to_all | solution.py:112
  24.4 8.4 %all-to-all-start.1 = ((f32[1,48,2304]{2,0,1:T(1,128)}), f32[1,48,2304]{2,0,1:T(1,128)S(1)}, u32[]{:S(2)}, u32[]{:S(2)}) async-start(f32[1,48,2304]{2,0,1:T(1,128)} %all_to_all.72), calls=%async_computation.1 | async-start | bytes 884736 | tf_op jit(solution)/shard_map/all_to_all | solution.py:113
  34.1 10.5 %all-to-all-done.1 = f32[1,48,2304]{2,0,1:T(1,128)S(1)} async-done(((f32[1,48,2304]{2,0,1:T(1,128)}), f32[1,48,2304]{2,0,1:T(1,128)S(1)}, u32[]{:S(2)}, u32[]{:S(2)}) %all-to-all-start.1) | async-done | bytes 442400 | tf_op jit(solution)/shard_map/all_to_all | solution.py:113
  48.4 5.8 %all-to-all-start.2 = ((f32[32,3,2304]{2,1,0:T(4,128)}), f32[32,3,2304]{2,1,0:T(4,128)S(1)}, u32[]{:S(2)}, u32[]{:S(2)}) async-start(f32[32,3,2304]{2,1,0:T(4,128)} %broadcast_select_fusion), calls=%async_computation.2 | async-start | bytes 2359296 | tf_op jit(solution)/shard_map/all_to_all | solution.py:115
  60.4 21.4 %all-to-all-done.2 = f32[32,3,2304]{2,1,0:T(4,128)S(1)} async-done(((f32[32,3,2304]{2,1,0:T(4,128)}), f32[32,3,2304]{2,1,0:T(4,128)S(1)}, u32[]{:S(2)}, u32[]{:S(2)}) %all-to-all-start.2) | async-done | bytes 884768 | tf_op jit(solution)/shard_map/all_to_all | solution.py:115
  83.2 2.7 %reshape.398 = f32[2,48,48,48]{3,2,0,1:T(8,128)S(1)} reshape(f32[2,16,3,2304]{3,0,2,1:T(2,128)} %bitcast.149) | data formatting | bytes 1769472 | tf_op jit(solution)/shard_map/reshape | solution.py:116
  85.9 3.6 %reshape.402 = f32[2,1,48,48,48]{4,3,0,2,1:T(8,128)} reshape(f32[2,16,3,2304]{3,0,2,1:T(2,128)} %bitcast.150) | data formatting | bytes 1769472 | tf_op jit(solution)/shard_map/reshape | solution.py:116
  89.6 3.0 %fusion.19 = f32[2,48,48,96]{3,2,1,0:T(8,128)S(1)} fusion(f32[2,48,48,48]{3,2,0,1:T(8,128)S(1)} %reshape.398, f32[2]{0:T(128)S(1)} %compare_convert_fusion, f32[48,48,48]{2,1,0:T(8,128)S(1)} %mul.413, f32[1,2,48,96]{3,2,0,1:T(8,128)} %get-tuple-element.25, f32[1,2,48,96]{3,2,0,1:T(8,128)} %get-tuple-element.24), kind=kOutput, calls=%fused_computation.23 | convolution fusion | flops 510068736 | bytes 3170312 | tf_op jit(solution)/shard_map/coxyz,cdzk->doxyk/dot_general | solution.py:45
  92.7 2.2 fusion.22
  94.9 2.7 %bitcast_multiply_fusion = f32[2,48,48,96]{3,1,2,0:T(8,128)S(1)} fusion(f32[2,48,48,96]{3,2,1,0:T(8,128)S(1)} %fusion.22, f32[48,48,96]{2,0,1:T(8,128)S(1)} %copy-done, f32[1,2,48,48]{2,3,0,1:T(8,128)S(1)} %copy-done.5, f32[1,2,48,48]{2,3,0,1:T(8,128)S(1)} %copy-done.6), kind=kOutput, calls=%fused_computation.7 | convolution fusion | flops 510059520 | bytes 4460544 | tf_op jit(solution)/shard_map/coxqk,cdxp->dopqk/dot_general | solution.py:51
  97.7 2.2 fusion.27
  99.9 2.7 %fusion.30 = f32[2,48,48,96]{3,2,1,0:T(8,128)S(1)} fusion(f32[2,48,48,96]{3,1,2,0:T(8,128)S(1)} %fusion.27, f32[1,2,48,48]{2,3,1,0:T(8,128)S(1)} %copy-done.4, f32[1,2,48,48]{2,3,1,0:T(8,128)S(1)} %copy-done.3), kind=kOutput, calls=%fused_computation.26 | convolution fusion | flops 509617152 | bytes 3575808 | tf_op jit(solution)/shard_map/coxqk,cdqy->doxyk/dot_general | solution.py:64
  102.6 3.0 %copy.111 = f32[2,1,48,48,48]{3,4,2,0,1:T(8,128)} copy(f32[2,1,48,48,48]{4,3,0,2,1:T(8,128)} %reshape.402) | data formatting | bytes 1769472 | tf_op jit(solution)/shard_map/reshape | solution.py:116
  105.6 8.1 %multiply_reduce_fusion = (f32[]{:T(128)}, f32[48,48,48]{1,2,0:T(8,128)S(1)}, f32[2,1,48,48,48]{3,4,2,0,1:T(8,128)}) fusion(f32[2,1,48,48,48]{3,4,2,0,1:T(8,128)} %copy.111, f32[2]{0:T(128)S(1)} %compare_convert_fusion, f32[48,48,48]{1,2,0:T(8,128)} %copy.119, f32[2,48,48,96]{3,2,1,0:T(8,128)S(1)} %fusion.30, f32[1,2,96,48]{2,3,0,1:T(8,128)} %get-tuple-element.21, ...), kind=kOutput, calls=%fused_computation.19 | convolution fusion | flops 510842880 | bytes 4497420 | tf_op jit(solution)/shard_map/coxyk,cdkz->doxyz/dot_general | solution.py:67
  119.8 28.6 %all_to_all.79 = f32[2,48,2304]{2,0,1:T(2,128)S(1)} all-to-all(f32[2,48,2304]{2,0,1:T(2,128)S(1)} %copy.114), channel_id=1, replica_groups=mesh['band_0'=2,'band_1'=8,'slab_0'=4,'slab_1'=2,'slab_2'=2] {'band_0','..., dimensions={1} | all-to-all | bytes 1769472 | tf_op jit(solution)/shard_map/all_to_all | solution.py:119
  150.3 5.7 %all-to-all-start.4 = ((f32[16,3,2304]{2,1,0:T(4,128)}), f32[16,3,2304]{2,1,0:T(4,128)}, u32[]{:S(2)}, u32[]{:S(2)}) async-start(f32[16,3,2304]{2,1,0:T(4,128)} %copy.117), calls=%async_computation.4 | async-start | bytes 1179648 | tf_op jit(solution)/shard_map/all_to_all | solution.py:120
  156.1 9.3 %all-reduce.1 = (f32[3,2304]{1,0:T(4,128)S(1)}, f32[]{:T(128)}) all-reduce(f32[3,2304]{1,0:T(4,128)S(1)} %multiply_reduce_fusion.2, f32[]{:T(128)} %get-tuple-element.10), channel_id=1, replica_groups=mesh['band_0'=2,'band_1'=8,'slab_0'=4,'slab_1'=2,'slab_2'=2] {'band_0'}, use_global_device_ids=true, to_apply=%region_1.0 | all-reduce | flops 6913 | bytes 55304 | tf_op jit(solution)/shard_map/psum | solution.py:23
  165.4 24.0 %all-reduce = (f32[3,2304]{1,0:T(4,128)}, f32[]{:T(128)}) all-reduce(f32[3,2304]{1,0:T(4,128)S(1)} %get-tuple-element.14, f32[]{:T(128)} %get-tuple-element.15), channel_id=1, replica_groups=mesh['band_0'=2,'band_1'=8,'slab_0'=4,'slab_1'=2,'slab_2'=2] {'band_1'}, use_global_device_ids=true, to_apply=%region_2.0 | all-reduce | flops 6913 | bytes 55304 | tf_op jit(solution)/shard_map/psum | solution.py:23
  189.4 7.1 %psum.53 = f32[]{:T(128)} all-reduce(f32[]{:T(128)} %get-tuple-element.13), channel_id=1, replica_groups=mesh['band_0'=2,'band_1'=8,'slab_0'=4,'slab_1'=2,'slab_2'=2] {'slab_0'}, use_global_device_ids=true, to_apply=%region_8.9 | all-reduce | flops 1 | bytes 8 | tf_op jit(solution)/shard_map/psum | solution.py:23
  196.5 5.9 %psum.54 = f32[]{:T(128)} all-reduce(f32[]{:T(128)} %psum.53), channel_id=1, replica_groups=mesh['band_0'=2,'band_1'=8,'slab_0'=4,'slab_1'=2,'slab_2'=2] {'slab_1'}, use_global_device_ids=true, to_apply=%region_9.10 | all-reduce | flops 1 | bytes 8 | tf_op jit(solution)/shard_map/psum | solution.py:23
  202.4 15.8 %psum.55 = f32[]{:T(128)} all-reduce(f32[]{:T(128)} %psum.54), channel_id=1, replica_groups=mesh['band_0'=2,'band_1'=8,'slab_0'=4,'slab_1'=2,'slab_2'=2] {'slab_2'}, use_global_device_ids=true, to_apply=%region_10.11 | all-reduce | flops 1 | bytes 8 | tf_op jit(solution)/shard_map/psum | solution.py:23
  222.4 5.1 %all-to-all-start.5 = ((f32[1,48,2304]{2,0,1:T(1,128)}), f32[1,48,2304]{2,0,1:T(1,128)S(1)}, u32[]{:S(2)}, u32[]{:S(2)}) async-start(f32[1,48,2304]{2,0,1:T(1,128)} %copy.118), calls=%async_computation.5 | async-start | bytes 884736 | tf_op jit(solution)/shard_map/all_to_all | solution.py:123
  227.6 10.2 %all-to-all-done.5 = f32[1,48,2304]{2,0,1:T(1,128)S(1)} async-done(((f32[1,48,2304]{2,0,1:T(1,128)}), f32[1,48,2304]{2,0,1:T(1,128)S(1)}, u32[]{:S(2)}, u32[]{:S(2)}) %all-to-all-start.5) | async-done | bytes 442400 | tf_op jit(solution)/shard_map/all_to_all | solution.py:123
  (69 shorter events, 32.0 us)
Async XLA Ops:
  2.8 20.3 %all-to-all-start = ((f32[16,3,2304]{2,1,0:T(4,128)}), f32[16,3,2304]{2,1,0:T(4,128)S(1)}, u32[]{:S(2)}, u32[]{:S(2)}) async-start(f32[16,3,2304]{2,1,0:T(4,128)} %copy.93), calls=%async_computation | async-start | bytes 1179648 | tf_op jit(solution)/shard_map/all_to_all | solution.py:112
  24.4 20.1 %all-to-all-start.1 = ((f32[1,48,2304]{2,0,1:T(1,128)}), f32[1,48,2304]{2,0,1:T(1,128)S(1)}, u32[]{:S(2)}, u32[]{:S(2)}) async-start(f32[1,48,2304]{2,0,1:T(1,128)} %all_to_all.72), calls=%async_computation.1 | async-start | bytes 884736 | tf_op jit(solution)/shard_map/all_to_all | solution.py:113
  48.4 33.5 %all-to-all-start.2 = ((f32[32,3,2304]{2,1,0:T(4,128)}), f32[32,3,2304]{2,1,0:T(4,128)S(1)}, u32[]{:S(2)}, u32[]{:S(2)}) async-start(f32[32,3,2304]{2,1,0:T(4,128)} %broadcast_select_fusion), calls=%async_computation.2 | async-start | bytes 2359296 | tf_op jit(solution)/shard_map/all_to_all | solution.py:115
  89.6 3.1 %copy-start.5 = (f32[1,2,48,48]{2,3,0,1:T(8,128)S(1)}, f32[1,2,48,48]{2,3,0,1:T(8,128)}, u32[]{:S(2)}) copy-start(f32[1,2,48,48]{2,3,0,1:T(8,128)} %get-tuple-element.17) | copy-start | bytes 55300
  89.6 3.1 %copy-start.6 = (f32[1,2,48,48]{2,3,0,1:T(8,128)S(1)}, f32[1,2,48,48]{2,3,0,1:T(8,128)}, u32[]{:S(2)}) copy-start(f32[1,2,48,48]{2,3,0,1:T(8,128)} %get-tuple-element.22) | copy-start | bytes 55300
  92.7 2.2 copy-start
  94.9 2.8 %copy-start.3 = (f32[1,2,48,48]{2,3,1,0:T(8,128)S(1)}, f32[1,2,48,48]{2,3,1,0:T(8,128)}, u32[]{:S(2)}) copy-start(f32[1,2,48,48]{2,3,1,0:T(8,128)} %get-tuple-element.16) | copy-start | bytes 55300
  94.9 2.8 %copy-start.4 = (f32[1,2,48,48]{2,3,1,0:T(8,128)S(1)}, f32[1,2,48,48]{2,3,1,0:T(8,128)}, u32[]{:S(2)}) copy-start(f32[1,2,48,48]{2,3,1,0:T(8,128)} %get-tuple-element.23) | copy-start | bytes 55300
  148.4 7.6 %copy-start.1 = (f32[16,3,2304]{2,0,1:T(8,128)S(1)}, f32[16,3,2304]{2,0,1:T(8,128)}, u32[]{:S(2)}) copy-start(f32[16,3,2304]{2,0,1:T(8,128)} %param.3) | copy-start | bytes 1327108
  150.3 69.5 %all-to-all-start.4 = ((f32[16,3,2304]{2,1,0:T(4,128)}), f32[16,3,2304]{2,1,0:T(4,128)}, u32[]{:S(2)}, u32[]{:S(2)}) async-start(f32[16,3,2304]{2,1,0:T(4,128)} %copy.117), calls=%async_computation.4 | async-start | bytes 1179648 | tf_op jit(solution)/shard_map/all_to_all | solution.py:120
  219.2 8.4 %copy-start.7 = (f32[3,2304]{1,0:T(4,128)S(1)}, f32[3,2304]{1,0:T(4,128)}, u32[]{:S(2)}) copy-start(f32[3,2304]{1,0:T(4,128)} %get-tuple-element.12) | copy-start | bytes 82948
  221.1 17.9 %copy-start.2 = (f32[16,3,2304]{2,0,1:T(8,128)S(1)}, f32[16,3,2304]{2,0,1:T(8,128)}, u32[]{:S(2)}) copy-start(f32[16,3,2304]{2,0,1:T(8,128)} %param.3) | copy-start | bytes 1327108
  222.4 15.4 %all-to-all-start.5 = ((f32[1,48,2304]{2,0,1:T(1,128)}), f32[1,48,2304]{2,0,1:T(1,128)S(1)}, u32[]{:S(2)}, u32[]{:S(2)}) async-start(f32[1,48,2304]{2,0,1:T(1,128)} %copy.118), calls=%async_computation.5 | async-start | bytes 884736 | tf_op jit(solution)/shard_map/all_to_all | solution.py:123
where the time goes:
time: 242 us; the launch traced here: 241 us
  blocking collectives  90.7 us (37%)
  waiting for transfers between devices  52 us (21%)
  starting transfers between devices  33.5 us (14%)
  local copies, waits for them, and re-layouts  30.4 us (13%)
  matrix products  21.5 us (9%)
  other arithmetic  10.6 us (4%)
  between operations  2.8 us (1%)
    psum x5, blocking collectives, over_axes(): return functools.reduce(lax.psum, axes, value)  62.1 us
    all_to_all x1, blocking collectives, body(): lax.all_to_all(outgoing, BAND, split_axis=1, concat_axis=0, tiled=True)  28.6 us
    all_to_all x1, waiting for transfers between devices, body(): lax.all_to_all(wanted, BAND, split_axis=0, concat_axis=1, tiled=True)  21.4 us
    all_to_all x1, waiting for transfers between devices, body(): lax.all_to_all(own_orbs, BAND, split_axis=1, concat_axis=0, tiled=True)  10.5 us
    all_to_all x1, waiting for transfers between devices, body(): lax.all_to_all(own_force + returned, SLAB, split_axis=1, concat_axis=0, t...  10.2 us
    all_to_all x1, waiting for transfers between devices, body(): lax.all_to_all(orbitals, SLAB, split_axis=0, concat_axis=1, tiled=True)  9.94 us
    reshape x3, local copies, waits for them, and re-layouts, body(): visitors = visitors.reshape((2, per_device) + own_orbs.shape[1:])  9.42 us
    all_to_all x1, starting transfers between devices, body(): lax.all_to_all(orbitals, SLAB, split_axis=0, concat_axis=1, tiled=True)  8.44 us
  transfers between devices with their start and end apart: 5, of which 4 were waited for; matrix products, arithmetic and copies ran while one was open for 4% of the time, Pallas kernels for 0%

commit v1 on v0

--- a/solution.py
+++ b/solution.py
@@ -110,7 +110,15 @@
     local_rows = slab_index * per_device + jnp.arange(per_device, dtype=jnp.int32)
     active = (local_rows[None, :] < my_counts[:, None]).astype(jnp.float32)
     own_orbs = lax.all_to_all(orbitals, SLAB, split_axis=0, concat_axis=1, tiled=True)
-    held_rows = lax.all_to_all(own_orbs, BAND, split_axis=1, concat_axis=0, tiled=True)
+    held_rows = jnp.concatenate(
+        lax.all_to_all(
+            jnp.stack(jnp.split(own_orbs, lax.axis_size(BAND), 1), 0),
+            axis_name=BAND,
+            split_axis=0,
+            concat_axis=0,
+        ),
+        0,
+    )
     wanted = request_rows(held_rows, partners, per_device)
     visitors = lax.all_to_all(wanted, BAND, split_axis=0, concat_axis=1, tiled=True)
     visitors = visitors.reshape((2, per_device) + own_orbs.shape[1:])

time: 242 us -> 242 us (level)
  no operation moved by 1% of the time
where the time goes in v1:
time: 242 us; the launch traced here: 241 us
  blocking collectives  90.7 us (37%)
  waiting for transfers between devices  52 us (21%)
  starting transfers between devices  33.4 us (14%)
  local copies, waits for them, and re-layouts  30.9 us (13%)
  matrix products  21.5 us (9%)
  other arithmetic  9.52 us (4%)
  between operations  2.88 us (1%)
    psum x5, blocking collectives, over_axes(): return functools.reduce(lax.psum, axes, value)  62.1 us
    all_to_all x1, blocking collectives, body(): lax.all_to_all(outgoing, BAND, split_axis=1, concat_axis=0, tiled=True)  28.6 us
    all_to_all x1, waiting for transfers between devices, body(): lax.all_to_all(wanted, BAND, split_axis=0, concat_axis=1, tiled=True)  21.4 us
    all_to_all x1, waiting for transfers between devices, body(): lax.all_to_all(jnp.stack(jnp.split(own_orbs, lax.axis_size(BAND), 1), 0),...  10.5 us
    all_to_all x1, waiting for transfers between devices, body(): lax.all_to_all(own_force + returned, SLAB, split_axis=1, concat_axis=0, t...  10.2 us
    all_to_all x1, waiting for transfers between devices, body(): lax.all_to_all(orbitals, SLAB, split_axis=0, concat_axis=1, tiled=True)  9.94 us
    reshape x3, local copies, waits for them, and re-layouts, body(): visitors = visitors.reshape((2, per_device) + own_orbs.shape[1:])  9.42 us
    all_to_all x1, starting transfers between devices, body(): lax.all_to_all(orbitals, SLAB, split_axis=0, concat_axis=1, tiled=True)  8.44 us
  transfers between devices with their start and end apart: 5, of which 4 were waited for; matrix products, arithmetic and copies ran while one was open for 4% of the time, Pallas kernels for 0%

profile of v1, /device:TPU:1, one launch (start us, length us, event | category | flops | bytes accessed | tf_op | source)
XLA Modules:
  0.0 241.0 jit_solution(6755862884331229820)
XLA Ops:
  2.8 8.4 %all-to-all-start = ((f32[16,3,2304]{2,1,0:T(4,128)}), f32[16,3,2304]{2,1,0:T(4,128)S(1)}, u32[]{:S(2)}, u32[]{:S(2)}) async-start(f32[16,3,2304]{2,1,0:T(4,128)} %copy.122), calls=%async_computation | async-start | bytes 1179648 | tf_op jit(solution)/shard_map/all_to_all | solution.py:112
  13.1 9.9 %all-to-all-done = f32[16,3,2304]{2,1,0:T(4,128)S(1)} async-done(((f32[16,3,2304]{2,1,0:T(4,128)}), f32[16,3,2304]{2,1,0:T(4,128)S(1)}, u32[]{:S(2)}, u32[]{:S(2)}) %all-to-all-start) | async-done | bytes 442400 | tf_op jit(solution)/shard_map/all_to_all | solution.py:112
  24.9 8.4 %all-to-all-start.1 = ((f32[16,1,3,2304]{3,1,2,0:T(1,128)}), f32[16,1,3,2304]{3,1,2,0:T(1,128)S(1)}, u32[]{:S(2)}, u32[]{:S(2)}) async-start(f32[16,1,3,2304]{3,1,2,0:T(1,128)} %copy.128), calls=%async_computation.1 | async-start | bytes 884736 | tf_op jit(solution)/shard_map/all_to_all | solution.py:114
  34.5 10.5 %all-to-all-done.1 = f32[16,1,3,2304]{3,1,2,0:T(1,128)S(1)} async-done(((f32[16,1,3,2304]{3,1,2,0:T(1,128)}), f32[16,1,3,2304]{3,1,2,0:T(1,128)S(1)}, u32[]{:S(2)}, u32[]{:S(2)}) %all-to-all-start.1) | async-done | bytes 442400 | tf_op jit(solution)/shard_map/all_to_all | solution.py:114
  47.9 5.8 %all-to-all-start.2 = ((f32[32,3,2304]{2,1,0:T(4,128)}), f32[32,3,2304]{2,1,0:T(4,128)S(1)}, u32[]{:S(2)}, u32[]{:S(2)}) async-start(f32[32,3,2304]{2,1,0:T(4,128)} %broadcast_select_fusion), calls=%async_computation.2 | async-start | bytes 2359296 | tf_op jit(solution)/shard_map/all_to_all | solution.py:123
  60.0 21.4 %all-to-all-done.2 = f32[32,3,2304]{2,1,0:T(4,128)S(1)} async-done(((f32[32,3,2304]{2,1,0:T(4,128)}), f32[32,3,2304]{2,1,0:T(4,128)S(1)}, u32[]{:S(2)}, u32[]{:S(2)}) %all-to-all-start.2) | async-done | bytes 884768 | tf_op jit(solution)/shard_map/all_to_all | solution.py:123
  82.8 2.7 %reshape.399 = f32[2,48,48,48]{3,2,0,1:T(8,128)S(1)} reshape(f32[2,16,3,2304]{3,0,2,1:T(2,128)} %bitcast.216) | data formatting | bytes 1769472 | tf_op jit(solution)/shard_map/reshape | solution.py:124
  85.5 3.6 %reshape.403 = f32[2,1,48,48,48]{4,3,0,2,1:T(8,128)} reshape(f32[2,16,3,2304]{3,0,2,1:T(2,128)} %bitcast.217) | data formatting | bytes 1769472 | tf_op jit(solution)/shard_map/reshape | solution.py:124
  89.1 3.0 %fusion.19 = f32[2,48,48,96]{3,2,1,0:T(8,128)S(1)} fusion(f32[2,48,48,48]{3,2,0,1:T(8,128)S(1)} %reshape.399, f32[2]{0:T(128)S(1)} %compare_convert_fusion, f32[48,48,48]{2,1,0:T(8,128)S(1)} %mul.413, f32[1,2,48,96]{3,2,0,1:T(8,128)} %get-tuple-element.27, f32[1,2,48,96]{3,2,0,1:T(8,128)} %get-tuple-element.26), kind=kOutput, calls=%fused_computation.23 | convolution fusion | flops 510068736 | bytes 3170312 | tf_op jit(solution)/shard_map/coxyz,cdzk->doxyk/dot_general | solution.py:45
  92.2 2.2 fusion.22
  94.5 2.7 %bitcast_multiply_fusion = f32[2,48,48,96]{3,1,2,0:T(8,128)S(1)} fusion(f32[2,48,48,96]{3,2,1,0:T(8,128)S(1)} %fusion.22, f32[48,48,96]{2,0,1:T(8,128)S(1)} %copy-done, f32[1,2,48,48]{2,3,0,1:T(8,128)S(1)} %copy-done.5, f32[1,2,48,48]{2,3,0,1:T(8,128)S(1)} %copy-done.6), kind=kOutput, calls=%fused_computation.7 | convolution fusion | flops 510059520 | bytes 4460544 | tf_op jit(solution)/shard_map/coxqk,cdxp->dopqk/dot_general | solution.py:51
  97.2 2.2 fusion.27
  99.4 2.7 %fusion.30 = f32[2,48,48,96]{3,2,1,0:T(8,128)S(1)} fusion(f32[2,48,48,96]{3,1,2,0:T(8,128)S(1)} %fusion.27, f32[1,2,48,48]{2,3,1,0:T(8,128)S(1)} %copy-done.4, f32[1,2,48,48]{2,3,1,0:T(8,128)S(1)} %copy-done.3), kind=kOutput, calls=%fused_computation.26 | convolution fusion | flops 509617152 | bytes 3575808 | tf_op jit(solution)/shard_map/coxqk,cdqy->doxyk/dot_general | solution.py:64
  102.1 3.0 %copy.142 = f32[2,1,48,48,48]{3,4,2,0,1:T(8,128)} copy(f32[2,1,48,48,48]{4,3,0,2,1:T(8,128)} %reshape.403) | data formatting | bytes 1769472 | tf_op jit(solution)/shard_map/reshape | solution.py:124
  105.2 8.1 %multiply_reduce_fusion = (f32[]{:T(128)}, f32[48,48,48]{1,2,0:T(8,128)S(1)}, f32[2,1,48,48,48]{3,4,2,0,1:T(8,128)}) fusion(f32[2,1,48,48,48]{3,4,2,0,1:T(8,128)} %copy.142, f32[2]{0:T(128)S(1)} %compare_convert_fusion, f32[48,48,48]{1,2,0:T(8,128)} %copy.150, f32[2,48,48,96]{3,2,1,0:T(8,128)S(1)} %fusion.30, f32[1,2,96,48]{2,3,0,1:T(8,128)} %get-tuple-element.23, ...), kind=kOutput, calls=%fused_computation.19 | convolution fusion | flops 510842880 | bytes 4497420 | tf_op jit(solution)/shard_map/coxyk,cdkz->doxyz/dot_general | solution.py:67
  119.3 28.6 %all_to_all.71 = f32[2,48,2304]{2,0,1:T(2,128)S(1)} all-to-all(f32[2,48,2304]{2,0,1:T(2,128)S(1)} %copy.145), channel_id=1, replica_groups=mesh['band_0'=2,'band_1'=8,'slab_0'=4,'slab_1'=2,'slab_2'=2] {'band_0','..., dimensions={1} | all-to-all | bytes 1769472 | tf_op jit(solution)/shard_map/all_to_all | solution.py:127
  149.8 5.7 %all-to-all-start.4 = ((f32[16,3,2304]{2,1,0:T(4,128)}), f32[16,3,2304]{2,1,0:T(4,128)}, u32[]{:S(2)}, u32[]{:S(2)}) async-start(f32[16,3,2304]{2,1,0:T(4,128)} %copy.148), calls=%async_computation.4 | async-start | bytes 1179648 | tf_op jit(solution)/shard_map/all_to_all | solution.py:128
  155.7 9.3 %all-reduce.1 = (f32[3,2304]{1,0:T(4,128)S(1)}, f32[]{:T(128)}) all-reduce(f32[3,2304]{1,0:T(4,128)S(1)} %multiply_reduce_fusion.2, f32[]{:T(128)} %get-tuple-element.12), channel_id=1, replica_groups=mesh['band_0'=2,'band_1'=8,'slab_0'=4,'slab_1'=2,'slab_2'=2] {'band_0'}, use_global_device_ids=true, to_apply=%region_1.0 | all-reduce | flops 6913 | bytes 55304 | tf_op jit(solution)/shard_map/psum | solution.py:23
  165.0 24.0 %all-reduce = (f32[3,2304]{1,0:T(4,128)}, f32[]{:T(128)}) all-reduce(f32[3,2304]{1,0:T(4,128)S(1)} %get-tuple-element.16, f32[]{:T(128)} %get-tuple-element.17), channel_id=1, replica_groups=mesh['band_0'=2,'band_1'=8,'slab_0'=4,'slab_1'=2,'slab_2'=2] {'band_1'}, use_global_device_ids=true, to_apply=%region_2.0 | all-reduce | flops 6913 | bytes 55304 | tf_op jit(solution)/shard_map/psum | solution.py:23
  188.9 7.1 %psum.53 = f32[]{:T(128)} all-reduce(f32[]{:T(128)} %get-tuple-element.15), channel_id=1, replica_groups=mesh['band_0'=2,'band_1'=8,'slab_0'=4,'slab_1'=2,'slab_2'=2] {'slab_0'}, use_global_device_ids=true, to_apply=%region_8.9 | all-reduce | flops 1 | bytes 8 | tf_op jit(solution)/shard_map/psum | solution.py:23
  196.1 5.9 %psum.54 = f32[]{:T(128)} all-reduce(f32[]{:T(128)} %psum.53), channel_id=1, replica_groups=mesh['band_0'=2,'band_1'=8,'slab_0'=4,'slab_1'=2,'slab_2'=2] {'slab_1'}, use_global_device_ids=true, to_apply=%region_9.10 | all-reduce | flops 1 | bytes 8 | tf_op jit(solution)/shard_map/psum | solution.py:23
  202.0 15.8 %psum.55 = f32[]{:T(128)} all-reduce(f32[]{:T(128)} %psum.54), channel_id=1, replica_groups=mesh['band_0'=2,'band_1'=8,'slab_0'=4,'slab_1'=2,'slab_2'=2] {'slab_2'}, use_global_device_ids=true, to_apply=%region_10.11 | all-reduce | flops 1 | bytes 8 | tf_op jit(solution)/shard_map/psum | solution.py:23
  222.0 5.1 %all-to-all-start.5 = ((f32[1,48,2304]{2,0,1:T(1,128)}), f32[1,48,2304]{2,0,1:T(1,128)S(1)}, u32[]{:S(2)}, u32[]{:S(2)}) async-start(f32[1,48,2304]{2,0,1:T(1,128)} %copy.149), calls=%async_computation.5 | async-start | bytes 884736 | tf_op jit(solution)/shard_map/all_to_all | solution.py:131
  227.2 10.2 %all-to-all-done.5 = f32[1,48,2304]{2,0,1:T(1,128)S(1)} async-done(((f32[1,48,2304]{2,0,1:T(1,128)}), f32[1,48,2304]{2,0,1:T(1,128)S(1)}, u32[]{:S(2)}, u32[]{:S(2)}) %all-to-all-start.5) | async-done | bytes 442400 | tf_op jit(solution)/shard_map/all_to_all | solution.py:131
  (86 shorter events, 31.5 us)
Async XLA Ops:
  2.8 20.3 %all-to-all-start = ((f32[16,3,2304]{2,1,0:T(4,128)}), f32[16,3,2304]{2,1,0:T(4,128)S(1)}, u32[]{:S(2)}, u32[]{:S(2)}) async-start(f32[16,3,2304]{2,1,0:T(4,128)} %copy.122), calls=%async_computation | async-start | bytes 1179648 | tf_op jit(solution)/shard_map/all_to_all | solution.py:112
  24.9 20.1 %all-to-all-start.1 = ((f32[16,1,3,2304]{3,1,2,0:T(1,128)}), f32[16,1,3,2304]{3,1,2,0:T(1,128)S(1)}, u32[]{:S(2)}, u32[]{:S(2)}) async-start(f32[16,1,3,2304]{3,1,2,0:T(1,128)} %copy.128), calls=%async_computation.1 | async-start | bytes 884736 | tf_op jit(solution)/shard_map/all_to_all | solution.py:114
  47.9 33.5 %all-to-all-start.2 = ((f32[32,3,2304]{2,1,0:T(4,128)}), f32[32,3,2304]{2,1,0:T(4,128)S(1)}, u32[]{:S(2)}, u32[]{:S(2)}) async-start(f32[32,3,2304]{2,1,0:T(4,128)} %broadcast_select_fusion), calls=%async_computation.2 | async-start | bytes 2359296 | tf_op jit(solution)/shard_map/all_to_all | solution.py:123
  89.1 3.1 %copy-start.5 = (f32[1,2,48,48]{2,3,0,1:T(8,128)S(1)}, f32[1,2,48,48]{2,3,0,1:T(8,128)}, u32[]{:S(2)}) copy-start(f32[1,2,48,48]{2,3,0,1:T(8,128)} %get-tuple-element.19) | copy-start | bytes 55300
  89.1 3.1 %copy-start.6 = (f32[1,2,48,48]{2,3,0,1:T(8,128)S(1)}, f32[1,2,48,48]{2,3,0,1:T(8,128)}, u32[]{:S(2)}) copy-start(f32[1,2,48,48]{2,3,0,1:T(8,128)} %get-tuple-element.24) | copy-start | bytes 55300
  92.2 2.2 copy-start
  94.4 2.8 %copy-start.3 = (f32[1,2,48,48]{2,3,1,0:T(8,128)S(1)}, f32[1,2,48,48]{2,3,1,0:T(8,128)}, u32[]{:S(2)}) copy-start(f32[1,2,48,48]{2,3,1,0:T(8,128)} %get-tuple-element.18) | copy-start | bytes 55300
  94.5 2.8 %copy-start.4 = (f32[1,2,48,48]{2,3,1,0:T(8,128)S(1)}, f32[1,2,48,48]{2,3,1,0:T(8,128)}, u32[]{:S(2)}) copy-start(f32[1,2,48,48]{2,3,1,0:T(8,128)} %get-tuple-element.25) | copy-start | bytes 55300
  147.9 7.7 %copy-start.1 = (f32[16,3,2304]{2,0,1:T(8,128)S(1)}, f32[16,3,2304]{2,0,1:T(8,128)}, u32[]{:S(2)}) copy-start(f32[16,3,2304]{2,0,1:T(8,128)} %param.3) | copy-start | bytes 1327108
  149.8 69.6 %all-to-all-start.4 = ((f32[16,3,2304]{2,1,0:T(4,128)}), f32[16,3,2304]{2,1,0:T(4,128)}, u32[]{:S(2)}, u32[]{:S(2)}) async-start(f32[16,3,2304]{2,1,0:T(4,128)} %copy.148), calls=%async_computation.4 | async-start | bytes 1179648 | tf_op jit(solution)/shard_map/all_to_all | solution.py:128
  218.7 8.3 %copy-start.7 = (f32[3,2304]{1,0:T(4,128)S(1)}, f32[3,2304]{1,0:T(4,128)}, u32[]{:S(2)}) copy-start(f32[3,2304]{1,0:T(4,128)} %get-tuple-element.14) | copy-start | bytes 82948
  220.7 17.9 %copy-start.2 = (f32[16,3,2304]{2,0,1:T(8,128)S(1)}, f32[16,3,2304]{2,0,1:T(8,128)}, u32[]{:S(2)}) copy-start(f32[16,3,2304]{2,0,1:T(8,128)} %param.3) | copy-start | bytes 1327108
  222.0 15.4 %all-to-all-start.5 = ((f32[1,48,2304]{2,0,1:T(1,128)}), f32[1,48,2304]{2,0,1:T(1,128)S(1)}, u32[]{:S(2)}, u32[]{:S(2)}) async-start(f32[1,48,2304]{2,0,1:T(1,128)} %copy.149), calls=%async_computation.5 | async-start | bytes 884736 | tf_op jit(solution)/shard_map/all_to_all | solution.py:131
